TPU v7x, 128 devices: a whole 4x4x4 slice. The times are simulated.
128 devices in a mesh: blk: 32 (over y, x, core), rep: 4 (over z).
Axes of the slice: x: 4, y: 4, z: 4, core: 2. Of those that a mesh axis runs over, the one named last changes fastest.
Arguments:
- anchors: float32 [3, 81920], P(None, ('blk', 'rep')), may hold values from -1 to 1
- directions: float32 [3, 81920], P(None, ('blk', 'rep')), may hold values from -4 to 4
- app_ids: int32 [81920], P(('blk', 'rep')), may hold values from 0 to 8191
- block_ids: int32 [640, 3], P(('blk', 'rep')), may hold values from 0 to 31, as said below
- color_grad: float32 [3, 81920], P(None, ('blk', 'rep')), may hold values from -6 to 6
- block_centers: float32 [3, 32], P(None, 'blk'), may hold values from -1 to 1
- pos_weight: bfloat16 [32, 256, 63], P('blk'), may hold values from -1 to 1
- trunk_weight: bfloat16 [32, 2, 256, 256], P('blk'), may hold values from -0.5 to 0.5
- density_weight: bfloat16 [32, 256], P('blk'), may hold values from -0.5 to 0.5
- feature_weight: bfloat16 [32, 128, 256], P('blk'), may hold values from -0.5 to 0.5
- view_weight: bfloat16 [32, 128, 27], P('blk'), may hold values from -1.25 to 1.25
- code_weight: bfloat16 [32, 128, 32], P('blk'), may hold values from -1 to 1
- radiance_weight: bfloat16 [32, 3, 128], P('blk'), may hold values from -0.75 to 0.75
- code_table: bfloat16 [32, 32, 8192], P('blk'), may hold values from -5 to 5
Outputs:
- colors: float32 [3, 81920], P(None, ('blk', 'rep'))
- grad_pos_weight: float32 [32, 256, 63], P('blk')
- grad_trunk_weight: float32 [32, 2, 256, 256], P('blk')
- grad_density_weight: float32 [32, 256], P('blk')
- grad_feature_weight: float32 [32, 128, 256], P('blk')
- grad_view_weight: float32 [32, 128, 27], P('blk')
- grad_code_weight: float32 [32, 128, 32], P('blk')
- grad_radiance_weight: float32 [32, 3, 128], P('blk')
- grad_code_table: float32 [32, 32, 8192], P('blk')
Inputs may be any that keep to these rules, and one draw needn't show every extreme that they name: `block_ids`: each tile names three different blocks; the tiles of one device never name the same block twice; among the devices that share an index along rep, every block is named by at most 30 tiles, and some block by exactly 30 tiles.
All inputs are finite; a program needn't handle non-finite values.
Results may differ from a plain program's by a relative error of at most 0.015.
Values sent between devices are 32-bit elements; how exact they have to be, the bound alone decides.
A program may use at most 64 MiB of HBM per device.

v0:
```python
import math

import jax
import jax.numpy as jnp
from jax import lax
from jax.sharding import PartitionSpec as P

TILE = 128
SAMPLES = 4
FREQ = 10
VFREQ = 4


ray_span = 2.0
loss_scale = 0.03125


def in_one_piece(arrays, axis, split_dim, concat_dim, along):
    widths = [math.prod(a.shape[along:]) for a in arrays]
    both = jnp.concatenate(
        [a.reshape(*a.shape[:along], w) for a, w in zip(arrays, widths)], axis=along
    )
    out = lax.all_to_all(both, axis, split_axis=split_dim, concat_axis=concat_dim, tiled=True)
    blocks = jnp.split(out, [sum(widths[:k]) for k in range(1, len(widths))], axis=along)
    return tuple((b.reshape(*out.shape[:along], *a.shape[along:]) for a, b in zip(arrays, blocks)))


def encode(values, levels):
    scales = 2.0 ** jnp.arange(levels, dtype=jnp.float32)
    angles = (scales[:, None, None] * values[None]).reshape(levels * 3, values.shape[1])
    return jnp.concatenate([values, jnp.sin(angles), jnp.cos(angles)], 0)


def render(params, code_block, center, anchor, direction, codes_row):
    (
        pos_weight,
        trunk_weight,
        density_weight,
        feature_weight,
        view_weight,
        code_weight,
        radiance_weight,
    ) = params
    ray_count = anchor.shape[1]
    spacing = ray_span / SAMPLES
    depths = (jnp.arange(SAMPLES, dtype=jnp.float32) + 0.5) * spacing
    points = (
        anchor[:, None, :] + depths[None, :, None] * direction[:, None, :] - center[:, None, None]
    )
    points = points.reshape(3, SAMPLES * ray_count)
    pos_code = encode(points, FREQ).astype(jnp.bfloat16)
    hidden = jax.nn.softplus(
        jnp.dot(pos_weight, pos_code, preferred_element_type=jnp.float32)
    ).astype(jnp.bfloat16)
    for level_index in range(trunk_weight.shape[0]):
        hidden = jax.nn.softplus(
            jnp.dot(trunk_weight[level_index], hidden, preferred_element_type=jnp.float32)
        ).astype(jnp.bfloat16)
    density = jax.nn.softplus(
        jnp.dot(density_weight[None, :], hidden, preferred_element_type=jnp.float32)
    ).reshape(SAMPLES, ray_count)
    view_code = encode(direction, VFREQ).astype(jnp.bfloat16)
    app_code = jnp.take(code_block, codes_row, axis=1)
    per_ray = jnp.dot(view_weight, view_code, preferred_element_type=jnp.float32) + jnp.dot(
        code_weight, app_code, preferred_element_type=jnp.float32
    )
    feature = jnp.dot(feature_weight, hidden, preferred_element_type=jnp.float32).reshape(
        -1, SAMPLES, ray_count
    )
    shaded = (
        jax.nn.softplus(feature + per_ray[:, None, :])
        .astype(jnp.bfloat16)
        .reshape(-1, SAMPLES * ray_count)
    )
    radiance = jax.nn.sigmoid(
        jnp.dot(radiance_weight, shaded, preferred_element_type=jnp.float32)
    ).reshape(3, SAMPLES, ray_count)
    optical = density * spacing
    passed = jnp.exp(-(jnp.cumsum(optical, 0) - optical))
    sample_weight = passed * (1.0 - jnp.exp(-optical))
    ray_color = jnp.sum(sample_weight[None] * radiance, 1)
    opacity = jnp.sum(sample_weight, 0)
    offset = anchor - center[:, None]
    blend_weight = (0.1 + opacity) / (1.0 + jnp.sum(offset * offset, 0))
    return jnp.concatenate([ray_color * blend_weight[None], blend_weight[None]], 0)


def blend_colors(partials):
    return partials[:, :3] / partials[:, 3:4]


def compact(flags, capacity):
    slot_rank = jnp.cumsum(flags) - 1
    live_count = jnp.sum(flags)
    wanted = jnp.arange(capacity, dtype=jnp.int32)
    hit_table = (flags[None, :] > 0) & (slot_rank[None, :] == wanted[:, None])
    picked = jnp.sum(
        jnp.where(hit_table, jnp.arange(flags.shape[0], dtype=jnp.int32)[None, :], 0), 1
    )
    is_valid = (wanted < live_count).astype(jnp.float32)
    return (picked, jnp.clip(slot_rank, 0, capacity - 1), is_valid)


def local(
    anchors,
    directions,
    app_ids,
    block_ids,
    color_grad,
    block_centers,
    pos_weight,
    trunk_weight,
    density_weight,
    feature_weight,
    view_weight,
    code_weight,
    radiance_weight,
    code_table,
):
    tile_count = block_ids.shape[0]
    capacity = min(lax.axis_size("blk"), 6 * tile_count)
    ray_tiles = (
        jnp.concatenate([anchors, directions], 0).reshape(6, tile_count, TILE).transpose(1, 0, 2)
    )
    code_tiles = app_ids.reshape(tile_count, TILE)
    grad_tiles = color_grad.reshape(3, tile_count, TILE).transpose(1, 0, 2)
    params = tuple(
        (
            member[0]
            for member in (
                pos_weight,
                trunk_weight,
                density_weight,
                feature_weight,
                view_weight,
                code_weight,
                radiance_weight,
            )
        )
    )
    code_block = code_table[0]
    center = block_centers[:, 0]

    def forward_tile(inputs):
        ray_rows, codes_row = inputs
        return render(params, code_block, center, ray_rows[:3], ray_rows[3:], codes_row)

    peer_index = jnp.arange(lax.axis_size("blk"), dtype=jnp.int32)
    flat_ids = block_ids.reshape(-1)
    matches = (flat_ids[None, :] == peer_index[:, None]).astype(jnp.int32)
    is_live = jnp.sum(matches, 1)
    source_tile = jnp.sum(matches * jnp.arange(flat_ids.shape[0], dtype=jnp.int32)[None, :], 1) // 3
    live_scale = is_live.astype(jnp.float32)
    send_rays = ray_tiles[source_tile] * live_scale[:, None, None]
    send_codes = code_tiles[source_tile] * is_live[:, None]
    got_rays, got_codes, got_live = (
        lax.all_to_all(send_rays, "blk", split_axis=0, concat_axis=0, tiled=True),
        *in_one_piece((send_codes, is_live), "blk", 0, 0, 1),
    )
    picked, slot_rank, is_valid = compact(got_live, capacity)
    my_rays = got_rays[picked]
    my_codes = got_codes[picked]
    partials = lax.map(forward_tile, (my_rays, my_codes))
    back_parts = partials[slot_rank] * got_live.astype(jnp.float32)[:, None, None]
    returned = lax.all_to_all(back_parts, "blk", split_axis=0, concat_axis=0, tiled=True)
    summed = returned[block_ids[:, 0]] + returned[block_ids[:, 1]] + returned[block_ids[:, 2]]
    ray_colors, pullback = jax.vjp(blend_colors, summed)
    (cot_parts,) = pullback(grad_tiles * loss_scale)
    send_cot = cot_parts[source_tile] * live_scale[:, None, None]
    got_cot = lax.all_to_all(send_cot, "blk", split_axis=0, concat_axis=0, tiled=True)
    my_cot = got_cot[picked]
    my_cot = my_cot * is_valid[:, None, None]
    earlier_rows = jnp.tril(jnp.ones((TILE, TILE), jnp.bool_), -1)

    def backward_tile(totals, inputs):
        ray_rows, codes_row, cot_row = inputs

        def local_render(weights, table_block):
            return render(weights, table_block, center, ray_rows[:3], ray_rows[3:], codes_row)

        _, pull_back = jax.vjp(local_render, params, code_block)
        grad_params, grad_block = pull_back(cot_row)
        pieces = tuple(grad_params) + (grad_block,)
        repeated = jnp.any((codes_row[:, None] == codes_row[None, :]) & earlier_rows, 1)
        first_seen = 1.0 - repeated.astype(jnp.float32)
        columns = jnp.take(grad_block, codes_row, axis=1).astype(jnp.float32) * first_seen[None, :]
        return (
            tuple(
                (
                    running + piece_grad.astype(jnp.float32)
                    for running, piece_grad in zip(totals, pieces)
                )
            ),
            columns,
        )

    start = tuple((jnp.zeros(member.shape, jnp.float32) for member in params + (code_block,)))
    totals, tile_columns = lax.scan(backward_tile, start, (my_rays, my_codes, my_cot))
    totals = lax.psum(totals, "rep")
    colors = ray_colors.transpose(1, 0, 2).reshape(3, tile_count * TILE)
    return (
        colors,
        totals[0][None],
        totals[1][None],
        totals[2][None],
        totals[3][None],
        totals[4][None],
        totals[5][None],
        totals[6][None],
        totals[7][None],
    )


def solution(mesh):
    return jax.shard_map(
        local,
        mesh=mesh,
        in_specs=(
            P(None, ("blk", "rep")),
            P(None, ("blk", "rep")),
            P(("blk", "rep")),
            P(("blk", "rep"), None),
            P(None, ("blk", "rep")),
            P(None, "blk"),
            P("blk", None, None),
            P("blk", None, None, None),
            P("blk", None),
            P("blk", None, None),
            P("blk", None, None),
            P("blk", None, None),
            P("blk", None, None),
            P("blk", None, None),
        ),
        out_specs=(
            P(None, ("blk", "rep")),
            P("blk", None, None),
            P("blk", None, None, None),
            P("blk", None),
            P("blk", None, None),
            P("blk", None, None),
            P("blk", None, None),
            P("blk", None, None),
            P("blk", None, None),
        ),
        check_vma=False,
    )
```

profile of v0, /device:TPU:1, one launch (start us, length us, event | category | flops | bytes accessed | tf_op | source)
XLA Modules:
  0.0 1040.3 jit_solution(18313090935815652111)
XLA Ops:
  10.0 8.6 all-to-all-start.1
  23.2 2.7 copy.63
  25.9 7.4 all-to-all-start
  35.1 5.8 all-to-all-done
  41.6 186.4 %while.35 = (s32[]{:T(128)}, f32[30,4,128]{2,1,0:T(4,128)S(1)}, f32[30,6,128]{2,1,0:T(8,128)S(1)}, f32[3,1]{0,1:T(1,128)S(1)}, bf16[256,63]{1,0:T(8,128)(2,1)S(1...) while((s32[]{:T(128)}, f32[30,4,128]{2,1,0:T(4,128)S(1)}, ...), condition=%wide.region_9.10_spmd, body=%wide.region_4.9_spmd.sunk | while | flops 190467712 | bytes 3034609 | solution.py:163
  48.6 2.5 gather_fusion
  54.8 2.5 gather_fusion
  67.2 2.5 gather_fusion
  229.4 3.9 all-to-all-start.2
  233.3 7.4 all-to-all-done.2
  244.5 3.9 all-to-all-start.3
  249.3 6.5 all-to-all-done.3
  256.5 665.5 %while.36 = (s32[]{:T(128)}, f32[256,63]{0,1:T(8,128)S(1)}, f32[2,256,256]{2,1,0:T(8,128)S(1)}, f32[256]{0:T(256)S(1)}, f32[128,256]{1,0:T(8,128)S(1)}, /*index=...) while((s32[]{:T(128)}, f32[256,63]{0,1:T(8,128)S(1)}, ...), condition=%wide.region_22.24_spmd.clone, body=%wide.region_12.23_spmd.clone.sunk | while | flops 558246912 | bytes 17397472 | solution.py:198
  277.2 2.5 gather_fusion.1
  293.8 4.7 select_add_fusion.8
  299.3 2.5 gather_fusion.1
  315.8 4.7 select_add_fusion.8
  337.8 4.7 select_add_fusion.8
  343.3 2.5 gather_fusion.1
  359.8 4.7 select_add_fusion.8
  381.9 4.7 select_add_fusion.8
  403.9 4.7 select_add_fusion.8
  425.9 4.7 select_add_fusion.8
  448.0 4.7 select_add_fusion.8
  470.0 4.7 select_add_fusion.8
  492.0 4.7 select_add_fusion.8
  514.0 4.7 select_add_fusion.8
  536.1 4.7 select_add_fusion.8
  558.1 4.7 select_add_fusion.8
  580.1 4.7 select_add_fusion.8
  602.6 4.7 select_add_fusion.8
  625.1 4.7 select_add_fusion.8
  647.6 4.7 select_add_fusion.8
  670.1 4.7 select_add_fusion.8
  692.6 4.7 select_add_fusion.8
  715.0 4.7 select_add_fusion.8
  737.5 4.7 select_add_fusion.8
  760.0 4.7 select_add_fusion.8
  782.5 4.7 select_add_fusion.8
  805.0 4.7 select_add_fusion.8
  827.5 4.7 select_add_fusion.8
  849.9 4.7 select_add_fusion.8
  872.4 4.7 select_add_fusion.8
  894.9 4.7 select_add_fusion.8
  917.4 4.7 select_add_fusion.8
  924.0 3.6 copy.65
  927.7 34.7 %all-reduce.9.cloned.1.call-done = (f32[1,256,63]{1,0,2:T(1,128)}, f32[1,256]{1,0:T(1,128)}, f32[1,128,27]{1,0,2:T(1,128)}, f32[1,128,32]{1,2,0:T(8,128)}, f32[1,3,128]{2,0,1:T(1,128)}) async-done(((f32[1,256,63]{1,0,2:T(1,128)}, f32[1,256]{1,0:T(1,128)}, f32[1,128,27]{1,0,2:T(1,128)}, f32[1,128,32]{1,2,0:T(8,128)}, f32[1,3,128]{2,0,1:T(1,128)}), (f32[1,256,63]{1,0,2:T(1,128)}, f32[1,256]{1,0:T(1,128)}, ...) | async-done | bytes 97296 | tf_op jit(solution)/shard_map/psum | solution.py:199
  962.4 58.9 %all-reduce.11.cloned.1.call-done = (f32[1,2,256,256]{3,2,1,0:T(8,128)}, f32[1,128,256]{2,1,0:T(8,128)}, f32[1,32,8192]{2,1,0:T(8,128)}) async-done(((f32[1,2,256,256]{3,2,1,0:T(8,128)}, f32[1,128,256]{2,1,0:T(8,128)}, f32[1,32,8192]{2,1,0:T(8,128)}), (f32[1,2,256,256]{3,2,1,0:T(8,128)}, f32[1,128,256]{2,1,0:T(8,128)}, f32[1,32,8192]{2,1,0:T(8,128)})) %all-reduce.11.cloned.1.call-update) | async-done | bytes 1703952 | tf_op jit(solution)/shard_map/psum | solution.py:199
  (3219 shorter events, 720.4 us)
Async XLA Ops:
  7.2 1.4 copy-start
  7.2 34.3 %copy-start.5 = (bf16[1,256]{1,0:T(2,128)(2,1)S(1)}, bf16[1,256]{1,0:T(2,128)(2,1)}, u32[]{:S(2)}) copy-start(bf16[1,256]{1,0:T(2,128)(2,1)} %param.27) | copy-start | bytes 1540
  7.2 34.3 %copy-start.6 = (f32[3,1]{0,1:T(1,128)S(1)}, f32[3,1]{0,1:T(1,128)}, u32[]{:S(2)}) copy-start(f32[3,1]{0,1:T(1,128)} %param.24) | copy-start | bytes 40
  7.2 34.3 %copy-start.9 = (bf16[1,3,128]{2,1,0:T(4,128)(2,1)S(1)}, bf16[1,3,128]{2,1,0:T(4,128)(2,1)}, u32[]{:S(2)}) copy-start(bf16[1,3,128]{2,1,0:T(4,128)(2,1)} %param.31) | copy-start | bytes 2308
  7.2 34.3 %copy-start.4 = (bf16[1,128,27]{1,2,0:T(8,128)(2,1)S(1)}, bf16[1,128,27]{1,2,0:T(8,128)(2,1)}, u32[]{:S(2)}) copy-start(bf16[1,128,27]{1,2,0:T(8,128)(2,1)} %param.29) | copy-start | bytes 20740
  7.2 34.3 %copy-start.3 = (bf16[1,128,256]{2,1,0:T(8,128)(2,1)S(1)}, bf16[1,128,256]{2,1,0:T(8,128)(2,1)}, u32[]{:S(2)}) copy-start(bf16[1,128,256]{2,1,0:T(8,128)(2,1)} %param.28) | copy-start | bytes 196612
  7.2 34.3 %copy-start.11 = (bf16[1,2,256,256]{3,2,1,0:T(8,128)(2,1)S(1)}, bf16[1,2,256,256]{3,2,1,0:T(8,128)(2,1)}, u32[]{:S(2)}) copy-start(bf16[1,2,256,256]{3,2,1,0:T(8,128)(2,1)} %param.26) | copy-start | bytes 786436
  10.0 15.9 %all-to-all-start.1 = ((s32[32,1,129]{2,1,0:T(1,128)}), s32[32,1,129]{2,1,0:T(1,128)S(1)}, u32[]{:S(2)}, u32[]{:S(2)}) async-start(s32[32,1,129]{2,1,0:T(1,128)} %copy.61), calls=%async_computation.1 | async-start | bytes 65536 | tf_op jit(solution)/shard_map/all_to_all | solution.py:23
  25.9 15.0 %all-to-all-start = ((f32[32,6,128]{2,1,0:T(8,128)}), f32[32,6,128]{2,1,0:T(8,128)S(1)}, u32[]{:S(2)}, u32[]{:S(2)}) async-start(f32[32,6,128]{2,1,0:T(8,128)} %broadcast_multiply_fusion.1), calls=%async_computation | async-start | bytes 262144 | tf_op jit(solution)/shard_map/all_to_all | solution.py:157
  41.6 200.9 %copy-start.7 = (f32[3,640]{1,0:T(4,128)S(1)}, f32[3,640]{1,0:T(4,128)}, u32[]{:S(2)}) copy-start(f32[3,640]{1,0:T(4,128)} %param.23) | copy-start | bytes 23044
  229.4 11.4 %all-to-all-start.2 = ((f32[32,4,128]{2,1,0:T(4,128)}), f32[32,4,128]{2,1,0:T(4,128)S(1)}, u32[]{:S(2)}, u32[]{:S(2)}) async-start(f32[32,4,128]{2,1,0:T(4,128)} %broadcast_multiply_fusion.3), calls=%async_computation.2 | async-start | bytes 131072 | tf_op jit(solution)/shard_map/all_to_all | solution.py:165
  244.5 11.3 %all-to-all-start.3 = ((f32[32,4,128]{2,1,0:T(4,128)}), f32[32,4,128]{2,1,0:T(4,128)S(1)}, u32[]{:S(2)}, u32[]{:S(2)}) async-start(f32[32,4,128]{2,1,0:T(4,128)} %broadcast_multiply_fusion.2), calls=%async_computation.3 | async-start | bytes 131072 | tf_op jit(solution)/shard_map/all_to_all | solution.py:170
  248.4 714.0 %all-reduce.9.cloned.1.call-start = ((), (), s32[]{:S(2)}) async-start(), calls=%async_computation.4 | async-start | bytes 194560 | tf_op jit(solution)/shard_map/psum | solution.py:199
  922.1 1.9 copy-start.8
  922.1 1.9 copy-start.10
  922.1 5.6 copy-start.1
  922.1 5.6 copy-start.2
  924.0 97.2 %all-reduce.11.cloned.1.call-start = ((), (), s32[]{:S(2)}) async-start(), calls=%async_computation.5 | async-start | bytes 3407872 | tf_op jit(solution)/shard_map/psum | solution.py:199
Sparse Core Ops, SparseCore 0:
  924.1 38.2 all-reduce.8
  966.1 55.0 all-reduce.10
where the time goes:
time: 1050 us; the launch traced here: 1040 us
  matrix products  392 us (37%)
  other arithmetic  270 us (26%)
  local copies, waits for them, and re-layouts  214 us (20%)
  waiting for transfers between devices  113 us (11%)
  starting transfers between devices  24 us (2%)
  between operations  14.4 us (1%)
  loops' own time  11.8 us (1%)
    dot_general x180, matrix products, render(): jnp.dot(trunk_weight[level_index], hidden, preferred_element_type=jnp.flo...  177 us
    gather x60, local copies, waits for them, and re-layouts, render(): app_code = jnp.take(code_block, codes_row, axis=1)  150 us
    add x90, other arithmetic, backward_tile(): running + piece_grad.astype(jnp.float32)  142 us
    psum x2, waiting for transfers between devices, local(): totals = lax.psum(totals, 'rep')  93.5 us
    dot_general x90, matrix products, render(): jnp.dot(feature_weight, hidden, preferred_element_type=jnp.float32)  85.9 us
    scatter-add x30, other arithmetic, render(): app_code = jnp.take(code_block, codes_row, axis=1)  62.7 us
    dot_general x90, matrix products, render(): jnp.dot(pos_weight, pos_code, preferred_element_type=jnp.float32)  41.7 us
    dot_general x120, matrix products, render(): jnp.dot(radiance_weight, shaded, preferred_element_type=jnp.float32)  32.5 us
  transfers between devices with their start and end apart: 6, of which 5 were waited for; matrix products, arithmetic and copies ran while one was open for 1% of the time, Pallas kernels for 0%

commit v1 on v0

v1 whole, which is shorter than its diff:
```python
import numpy as np

import jax
import jax.numpy as jnp
from jax import lax
from jax.experimental import pallas as pl
from jax.experimental.pallas import tpu as pltpu
from jax.sharding import PartitionSpec as P

TILE = 128
SAMPLES = 4
SLOTS = 32
LANES = SAMPLES * TILE
HID = 256
CHID = 128
PC = 96
VC = 48
E = 32
RC = VC + E
LO = 256
SPACING = 0.5
LOSS_SCALE = 0.03125
LOG2E = 1.4426950408889634
LN2 = 0.6931471805599453

R_H1 = PC
R_H2 = R_H1 + HID
R_H3 = R_H2 + HID
R_S = R_H3 + HID
R_END = R_S + CHID

G_T1 = 0
G_T2 = 256
G_FD = 512
G_TAB = 656
G_POS = 1680
G_ROWS = 1984


def code_places(levels, half):
    raw = list(range(3))
    sines, cosines = [], []
    for level in range(levels):
        for c in range(3):
            row = (level // half) * 3 + c
            group = 2 * (level % half)
            sines.append(8 * (1 + group) + row)
            cosines.append(8 * (2 + group) + row)
    return raw + sines + cosines


def selection(places, width):
    out = np.zeros((len(places), width), np.float32)
    out[np.arange(len(places)), places] = 1.0
    return out


POS_SELECT = selection(code_places(10, 5), PC)
VIEW_SELECT = selection(code_places(4, 2), VC)


def mm(a, b):
    return lax.dot_general(a, b, (((1,), (0,)), ((), ())), preferred_element_type=jnp.float32)


def mm_nt(a, b):
    return lax.dot_general(a, b, (((1,), (1,)), ((), ())), preferred_element_type=jnp.float32)


def softplus(v):
    return jnp.maximum(v, 0.0) + jnp.log(1.0 + jnp.exp(-jnp.abs(v)))


def row_iota(rows, lanes):
    return lax.broadcasted_iota(jnp.int32, (rows, lanes), 0)


def ray_rows(ray, row):
    o8 = jnp.where(row < 3, ray, jnp.where(row < 6, pltpu.roll(ray, 3, 0), 0.0))
    d8 = jnp.where(row < 3, pltpu.roll(ray, 5, 0), jnp.where(row < 6, ray, 0.0))
    return o8, d8


def center_rows(center_ref, row):
    third = jnp.where(row >= 3, row - 3, row)
    return jnp.where(
        third == 0,
        center_ref[0, 0],
        jnp.where(third == 1, center_ref[1, 0], jnp.where(third == 2, center_ref[2, 0], 0.0)),
    )


def code_groups(values, doublings):
    groups = [values]
    sine, cosine = jnp.sin(values), jnp.cos(values)
    for step in range(doublings):
        groups += [sine, cosine]
        if step + 1 < doublings:
            sine, cosine = 2.0 * sine * cosine, (cosine - sine) * (cosine + sine)
    groups.append(jnp.zeros_like(values))
    return jnp.concatenate(groups, 0).astype(jnp.bfloat16)


def over_samples(x):
    return [x[:, s * TILE : (s + 1) * TILE] for s in range(SAMPLES)]


def composite(small, o8, c8, row):
    density = over_samples(softplus(small))
    rad = over_samples(1.0 / (1.0 + jnp.exp(-small)))
    off = o8 - c8
    off2 = jnp.sum(jnp.where(row < 3, off * off, 0.0), 0, keepdims=True)
    inv = 1.0 / (1.0 + off2)
    depth = jnp.zeros((1, TILE), jnp.float32)
    before = jnp.ones((1, TILE), jnp.float32)
    weights, after = [], []
    for s in range(SAMPLES):
        u = density[s][3:4] * SPACING
        weights.append(before * (1.0 - jnp.exp(-u)))
        depth = depth + u
        before = jnp.exp(-depth)
        after.append(before)
    color = sum(w * r for w, r in zip(weights, rad))
    opacity = sum(weights)
    return rad, weights, after, color, (0.1 + opacity) * inv, inv


def forward_kernel(
    live_ref, center_ref, rays_ref, pos_ref, trunk_ref, density_ref, feature_ref, view_ref,
    code_ref, radiance_ref, table_ref, pos_select_ref, view_select_ref,
    part_ref, saved_ref, raycode_ref, small_ref,
    wp, wfd, wray, wrad, tab, buf, sem,
):
    row = row_iota(8, TILE)
    c8 = center_rows(center_ref, row)
    wp[...] = mm(pos_ref[0], pos_select_ref[...]).astype(jnp.bfloat16)
    wray[:, :VC] = mm(view_ref[0], view_select_ref[...]).astype(jnp.bfloat16)
    wray[:, VC:] = code_ref[0]
    wfd[:CHID, :] = feature_ref[0]
    row16 = row_iota(16, HID)
    wfd[CHID:, :] = jnp.where(row16 == 3, density_ref[...].astype(jnp.float32), 0.0).astype(jnp.bfloat16)
    wrad[...] = jnp.concatenate(
        [radiance_ref[0].astype(jnp.float32), jnp.zeros((5, CHID), jnp.float32)], 0
    ).astype(jnp.bfloat16)
    for h in range(SLOTS):
        tab[h * E : (h + 1) * E, :] = table_ref[0, :, h * LO : (h + 1) * LO]
    pos_scale = jnp.where(row < 3, 1.0, 32.0)
    view_scale = jnp.where(row < 3, 1.0, 4.0)

    def saving(count):
        slot = count % 2
        return pltpu.make_async_copy(buf.at[slot], saved_ref.at[count], sem.at[slot])

    def tile(s, count):
        @pl.when(count >= 2)
        def _():
            saving(count - 2).wait()

        out = buf.at[count % 2]
        ray = rays_ref[s]
        o8, d8 = ray_rows(ray, row)
        points = jnp.concatenate(
            [(o8 + (t + 0.5) * SPACING * d8 - c8) * pos_scale for t in range(SAMPLES)], 1
        )
        out[:PC, :] = code_groups(points, 5)
        ids = ray[6:7].astype(jnp.int32)
        lo, hi = ids & (LO - 1), ids >> 8
        hot = (row_iota(LO, TILE) == lo).astype(jnp.float32).astype(jnp.bfloat16)
        rows = mm(tab[...], hot)
        app = jnp.zeros((E, TILE), jnp.float32)
        for h in range(SLOTS):
            app = app + jnp.where(hi == h, rows[h * E : (h + 1) * E], 0.0)
        raycode_ref[s, :VC, :] = code_groups(d8 * view_scale, 2)
        raycode_ref[s, VC:, :] = app.astype(jnp.bfloat16)
        per_ray = mm(wray[...], raycode_ref[s])
        out[R_H1:R_H2, :] = softplus(mm(wp[...], out[:PC, :])).astype(jnp.bfloat16)
        out[R_H2:R_H3, :] = softplus(mm(trunk_ref[0, 0], out[R_H1:R_H2, :])).astype(jnp.bfloat16)
        out[R_H3:R_S, :] = softplus(mm(trunk_ref[0, 1], out[R_H2:R_H3, :])).astype(jnp.bfloat16)
        both = mm(wfd[...], out[R_H3:R_S, :])
        out[R_S:R_END, :] = softplus(
            both[:CHID] + jnp.concatenate([per_ray] * SAMPLES, 1)
        ).astype(jnp.bfloat16)
        logits = mm(wrad[...], out[R_S:R_END, :])
        small = jnp.where(row_iota(8, LANES) == 3, both[CHID : CHID + 8], logits)
        small_ref[s] = small
        _, _, _, color, share, _ = composite(small, o8, c8, row)
        part_ref[s] = jnp.where(row < 3, color * share, share)[:4]
        saving(count).start()
        return count + 1

    def step(s, count):
        return lax.cond(live_ref[s] > 0, lambda: tile(s, count), lambda: count)

    count = lax.fori_loop(0, SLOTS, step, jnp.int32(0))

    @pl.when(count >= 2)
    def _():
        saving(count - 2).wait()

    @pl.when(count >= 1)
    def _():
        saving(count - 1).wait()


def backward_kernel(
    live_ref, center_ref, rays_ref, cot_ref, saved_ref, raycode_ref, small_ref, trunk_ref,
    density_ref, feature_ref, code_ref, radiance_ref,
    g_ref,
    t1, t2, fdt, codet, radt, buf, slots, sem,
):
    row = row_iota(8, TILE)
    c8 = center_rows(center_ref, row)

    def flip(x):
        return x.astype(jnp.float32).T.astype(jnp.bfloat16)

    t1[...] = flip(trunk_ref[0, 0])
    t2[...] = flip(trunk_ref[0, 1])
    fdt[:, :CHID] = flip(feature_ref[0])
    row16 = row_iota(16, HID)
    fdt[:, CHID:] = jnp.where(row16 == 3, density_ref[...].astype(jnp.float32), 0.0).T.astype(jnp.bfloat16)
    codet[...] = flip(code_ref[0])
    radt[...] = jnp.concatenate(
        [radiance_ref[0].astype(jnp.float32), jnp.zeros((13, CHID), jnp.float32)], 0
    ).T.astype(jnp.bfloat16)
    g_ref[...] = jnp.zeros_like(g_ref)

    def listing(s, count):
        @pl.when(live_ref[s] > 0)
        def _():
            slots[count] = s

        return count + (live_ref[s] > 0).astype(jnp.int32)

    total = lax.fori_loop(0, SLOTS, listing, jnp.int32(0))

    def fetching(j):
        return pltpu.make_async_copy(saved_ref.at[j], buf.at[j % 2], sem.at[j % 2])

    @pl.when(total > 0)
    def _():
        fetching(0).start()

    def tile(j, carry):
        s = slots[j]
        fetching(j).wait()

        @pl.when(j + 1 < total)
        def _():
            fetching(j + 1).start()

        act = buf.at[j % 2]
        ray = rays_ref[s]
        o8, _ = ray_rows(ray, row)
        small = small_ref[s]
        rad, weights, after, color, share, inv = composite(small, o8, c8, row)
        cot = jnp.concatenate([cot_ref[s], jnp.zeros((4, TILE), jnp.float32)], 0)
        d_share = jnp.sum(
            jnp.where(row < 3, cot * color, jnp.where(row == 3, cot, 0.0)), 0, keepdims=True
        )
        d_color = jnp.where(row < 3, cot * share, 0.0)
        d_opacity = d_share * inv
        sig = over_samples(1.0 / (1.0 + jnp.exp(-small)))
        later = jnp.zeros((1, TILE), jnp.float32)
        pieces = [None] * SAMPLES
        for t in reversed(range(SAMPLES)):
            d_w = jnp.sum(d_color * rad[t], 0, keepdims=True) + d_opacity
            d_u = d_w * after[t] - later
            later = later + d_w * weights[t]
            d_logit = d_color * weights[t] * rad[t] * (1.0 - rad[t])
            pieces[t] = jnp.where(
                row < 3, d_logit, jnp.where(row == 3, d_u * SPACING * sig[t], 0.0)
            )
        d_small = jnp.concatenate(pieces, 1)
        d_small = jnp.concatenate([d_small, jnp.zeros_like(d_small)], 0).astype(jnp.bfloat16)

        def through(grad, lo_row, hi_row):
            value = act[lo_row:hi_row, :].astype(jnp.float32)
            return grad * (1.0 - jnp.exp(-value))

        shaded = act[R_S:R_END, :]
        d_feature = through(mm(radt[...], d_small), R_S, R_END)
        g_ref[G_POS + CHID : G_POS + CHID + 16, 128:256] += mm_nt(d_small, shaded)
        d_ray = sum(over_samples(d_feature)).astype(jnp.bfloat16)
        g_ref[G_POS : G_POS + CHID, 128 : 128 + RC] += mm_nt(d_ray, raycode_ref[s])
        d_app = mm(codet[...], d_ray)
        ids = ray[6:7].astype(jnp.int32)
        lo, hi = ids & (LO - 1), ids >> 8
        hot = (row_iota(LO, TILE) == lo).astype(jnp.float32).astype(jnp.bfloat16)
        spread = jnp.concatenate(
            [jnp.where(hi == h, d_app, 0.0).astype(jnp.bfloat16) for h in range(SLOTS)], 0
        )
        g_ref[G_TAB:G_POS, :] += mm_nt(spread, hot)
        both = jnp.concatenate([d_feature.astype(jnp.bfloat16), d_small], 0)
        g_ref[G_FD:G_TAB, :] += mm_nt(both, act[R_H3:R_S, :])
        d_z = through(mm(fdt[...], both), R_H3, R_S).astype(jnp.bfloat16)
        g_ref[G_T2:G_FD, :] += mm_nt(d_z, act[R_H2:R_H3, :])
        d_z = through(mm(t2[...], d_z), R_H2, R_H3).astype(jnp.bfloat16)
        g_ref[G_T1:G_T2, :] += mm_nt(d_z, act[R_H1:R_H2, :])
        d_z = through(mm(t1[...], d_z), R_H1, R_H2).astype(jnp.bfloat16)
        g_ref[G_POS : G_POS + HID, :PC] += mm_nt(d_z, act[:PC, :])
        return carry

    lax.fori_loop(0, total, tile, jnp.int32(0))


def unpack_kernel(
    g_ref, pos_select_ref, view_select_ref,
    pos_ref, trunk_ref, density_ref, feature_ref, view_ref, code_ref, radiance_ref, table_ref,
):
    def pick(a, select):
        return lax.dot_general(
            a, select.astype(jnp.float32), (((1,), (1,)), ((), ())),
            preferred_element_type=jnp.float32, precision=lax.Precision.HIGHEST,
        )

    pos_ref[0] = pick(g_ref[G_POS : G_POS + HID, :PC], pos_select_ref[...])
    trunk_ref[0, 0] = g_ref[G_T1:G_T2, :]
    trunk_ref[0, 1] = g_ref[G_T2:G_FD, :]
    feature_ref[0] = g_ref[G_FD : G_FD + CHID, :]
    density_ref[...] = g_ref[G_FD + CHID + 3 : G_FD + CHID + 4, :]
    view_ref[0] = pick(g_ref[G_POS : G_POS + CHID, 128 : 128 + VC], view_select_ref[...])
    code_ref[0] = g_ref[G_POS : G_POS + CHID, 128 + VC : 128 + RC]
    radiance_ref[0] = g_ref[G_POS + CHID : G_POS + CHID + 3, 128:256]
    for h in range(SLOTS):
        table_ref[0, :, h * LO : (h + 1) * LO] = g_ref[G_TAB + h * E : G_TAB + (h + 1) * E, :]


VMEM = pl.BlockSpec(memory_space=pltpu.VMEM)
SMEM = pl.BlockSpec(memory_space=pltpu.SMEM)
ANY = pl.BlockSpec(memory_space=pl.ANY)


def run_forward(live, center, rays, pos, trunk, density, feature, view, code, radiance, table):
    bf = jnp.bfloat16
    return pl.pallas_call(
        forward_kernel,
        name="forward_tiles",
        out_shape=(
            jax.ShapeDtypeStruct((SLOTS, 4, TILE), jnp.float32),
            jax.ShapeDtypeStruct((SLOTS, R_END, LANES), bf),
            jax.ShapeDtypeStruct((SLOTS, RC, TILE), bf),
            jax.ShapeDtypeStruct((SLOTS, 8, LANES), jnp.float32),
        ),
        in_specs=[SMEM, SMEM] + [VMEM] * 11,
        out_specs=(VMEM, ANY, VMEM, VMEM),
        scratch_shapes=[
            pltpu.VMEM((HID, PC), bf),
            pltpu.VMEM((CHID + 16, HID), bf),
            pltpu.VMEM((CHID, RC), bf),
            pltpu.VMEM((8, CHID), bf),
            pltpu.VMEM((SLOTS * E, LO), bf),
            pltpu.VMEM((2, R_END, LANES), bf),
            pltpu.SemaphoreType.DMA((2,)),
        ],
        compiler_params=pltpu.CompilerParams(vmem_limit_bytes=32 * 1024 * 1024),
        cost_estimate=pl.CostEstimate(flops=10**10, bytes_accessed=3 * 10**7, transcendentals=0),
    )(live, center, rays, pos, trunk, density, feature, view, code, radiance, table,
      jnp.asarray(POS_SELECT, bf), jnp.asarray(VIEW_SELECT, bf))


def run_backward(live, center, rays, cot, saved, raycode, small, trunk, density, feature, code, radiance):
    bf = jnp.bfloat16
    return pl.pallas_call(
        backward_kernel,
        name="backward_tiles",
        out_shape=jax.ShapeDtypeStruct((G_ROWS, 256), jnp.float32),
        in_specs=[SMEM, SMEM, VMEM, VMEM, ANY] + [VMEM] * 7,
        out_specs=VMEM,
        scratch_shapes=[
            pltpu.VMEM((HID, HID), bf),
            pltpu.VMEM((HID, HID), bf),
            pltpu.VMEM((HID, CHID + 16), bf),
            pltpu.VMEM((E, CHID), bf),
            pltpu.VMEM((CHID, 16), bf),
            pltpu.VMEM((2, R_END, LANES), bf),
            pltpu.SMEM((SLOTS,), jnp.int32),
            pltpu.SemaphoreType.DMA((2,)),
        ],
        compiler_params=pltpu.CompilerParams(vmem_limit_bytes=32 * 1024 * 1024),
        cost_estimate=pl.CostEstimate(flops=2 * 10**10, bytes_accessed=3 * 10**7, transcendentals=0),
    )(live, center, rays, cot, saved, raycode, small, trunk, density, feature, code, radiance)


def run_unpack(packed):
    f32 = jnp.float32
    shapes = [(1, 256, 63), (1, 2, 256, 256), (1, 256), (1, 128, 256), (1, 128, 27), (1, 128, 32),
              (1, 3, 128), (1, 32, 8192)]
    return pl.pallas_call(
        unpack_kernel,
        name="unpack_gradients",
        out_shape=tuple(jax.ShapeDtypeStruct(s, f32) for s in shapes),
        in_specs=[VMEM] * 3,
        out_specs=tuple(VMEM for _ in shapes),
        compiler_params=pltpu.CompilerParams(vmem_limit_bytes=32 * 1024 * 1024),
    )(packed, jnp.asarray(POS_SELECT, jnp.bfloat16), jnp.asarray(VIEW_SELECT, jnp.bfloat16))


def local(
    anchors, directions, app_ids, block_ids, color_grad, block_centers, pos_weight, trunk_weight,
    density_weight, feature_weight, view_weight, code_weight, radiance_weight, code_table,
):
    tiles = block_ids.shape[0]
    peers = jnp.arange(SLOTS, dtype=jnp.int32)
    flat_ids = block_ids.reshape(-1)
    matches = (flat_ids[None, :] == peers[:, None]).astype(jnp.int32)
    is_live = jnp.sum(matches, 1)
    source_tile = jnp.sum(matches * jnp.arange(3 * tiles, dtype=jnp.int32)[None, :], 1) // 3
    rows = jnp.concatenate(
        [anchors, directions, app_ids.astype(jnp.float32)[None], jnp.zeros((1, tiles * TILE), jnp.float32)], 0
    )
    ray_tiles = rows.reshape(8, tiles, TILE).transpose(1, 0, 2)
    send = jnp.where(
        jnp.arange(8)[None, :, None] == 7,
        is_live.astype(jnp.float32)[:, None, None],
        ray_tiles[source_tile],
    )
    rays = lax.all_to_all(send, "blk", split_axis=0, concat_axis=0, tiled=True)
    live = (rays[:, 7, 0] > 0.5).astype(jnp.int32)
    part, saved, raycode, small = run_forward(
        live, block_centers, rays, pos_weight, trunk_weight, density_weight, feature_weight,
        view_weight, code_weight, radiance_weight, code_table,
    )
    returned = lax.all_to_all(part, "blk", split_axis=0, concat_axis=0, tiled=True)
    summed = returned[block_ids[:, 0]] + returned[block_ids[:, 1]] + returned[block_ids[:, 2]]
    scaled = color_grad.reshape(3, tiles, TILE).transpose(1, 0, 2) * LOSS_SCALE
    colors = summed[:, :3] / summed[:, 3:4]
    cot_color = scaled / summed[:, 3:4]
    cot = jnp.concatenate([cot_color, -jnp.sum(cot_color * colors, 1, keepdims=True)], 1)
    got_cot = lax.all_to_all(cot[source_tile], "blk", split_axis=0, concat_axis=0, tiled=True)
    packed = run_backward(
        live, block_centers, rays, got_cot, saved, raycode, small, trunk_weight, density_weight,
        feature_weight, code_weight, radiance_weight,
    )
    packed = lax.psum(packed, "rep")
    return (colors.transpose(1, 0, 2).reshape(3, tiles * TILE),) + tuple(run_unpack(packed))


def solution(mesh):
    weights = (P("blk", None, None), P("blk", None, None, None), P("blk", None)) + (
        P("blk", None, None),
    ) * 5
    ray = P(None, ("blk", "rep"))
    return jax.shard_map(
        local,
        mesh=mesh,
        in_specs=(ray, ray, P(("blk", "rep")), P(("blk", "rep"), None), ray, P(None, "blk")) + weights,
        out_specs=(ray,) + weights,
        check_vma=False,
    )
```

time: 1050 us -> 217 us (0.21)
  matrix products: 392 us -> 0 us
  other arithmetic: 270 us -> 4.47 us
  local copies, waits for them, and re-layouts: 214 us -> 17 us
  Pallas kernels: 0 us -> 49.1 us
  waiting for transfers between devices: 113 us -> 84.7 us
  loops' own time: 11.8 us -> 0 us
  blocking collectives: 0 us -> 10.9 us
  starting transfers between devices: 24 us -> 34.8 us
    dot_general x780 -> x0, matrix products: 392 us -> none  [the longest x180 177 us: render(): jnp.dot(trunk_weight[level_index], hidden, preferred_element_type=jnp.flo...]
    gather x67 -> x2, local copies, waits for them, and re-layouts: 154 us -> 1.19 us  [the longest x1 0.61 us: local(): cot[source_tile]]
    add x90 -> x0, other arithmetic: 142 us -> none  [backward_tile(): running + piece_grad.astype(jnp.float32)]
    scatter-add x30 -> x0, other arithmetic: 62.7 us -> none  [render(): app_code = jnp.take(code_block, codes_row, axis=1)]
    pallas_call x0 -> x3, Pallas kernels: none -> 49.1 us  [the longest x1 25.7 us: run_forward(): pl.pallas_call(forward_kernel, name='forward_tiles', out_shape=(jax.Shape...]
    another operation x331 -> x0, other arithmetic: 34.3 us -> none
    mul x540 -> x0, local copies, waits for them, and re-layouts: 26 us -> none  [the longest x480 21.8 us: encode(): scales[:, None, None] * values[None]]
    psum x2 -> x1, waiting for transfers between devices: 93.5 us -> 73.9 us  [local(): packed = lax.psum(packed, 'rep')]
  transfers between devices with their start and end apart: 6 -> 3, of which waited for: 5 -> 3; matrix products, arithmetic and copies ran while one was open for 1% -> 2% of each run, Pallas kernels for 0% -> 0%
where the time goes in v1:
time: 217 us; the launch traced here: 215 us
  waiting for transfers between devices  84.7 us (39%)
  Pallas kernels  49.1 us (23%)
  starting transfers between devices  34.8 us (16%)
  local copies, waits for them, and re-layouts  17 us (8%)
  between operations  14.2 us (7%)
  blocking collectives  10.9 us (5%)
  other arithmetic  4.47 us (2%)
    psum x1, waiting for transfers between devices, local(): packed = lax.psum(packed, 'rep')  73.9 us
    all_to_all x1, starting transfers between devices, local(): lax.all_to_all(part, 'blk', split_axis=0, concat_axis=0, tiled=True)  26.2 us
    pallas_call x1, Pallas kernels, run_forward(): pl.pallas_call(forward_kernel, name='forward_tiles', out_shape=(jax.Shape...  25.7 us
    pallas_call x1, Pallas kernels, run_backward(): pl.pallas_call(backward_kernel, name='backward_tiles', out_shape=jax.Shap...  22 us
    unnamed x40, local copies, waits for them, and re-layouts  13.9 us
    all_to_all x1, blocking collectives, local(): lax.all_to_all(cot[source_tile], 'blk', split_axis=0, concat_axis=0, tile...  10.9 us
    all_to_all x1, starting transfers between devices, local(): rays = lax.all_to_all(send, 'blk', split_axis=0, concat_axis=0, tiled=True)  8.58 us
    all_to_all x1, waiting for transfers between devices, local(): lax.all_to_all(part, 'blk', split_axis=0, concat_axis=0, tiled=True)  7.26 us
  transfers between devices with their start and end apart: 3, of which 3 were waited for; matrix products, arithmetic and copies ran while one was open for 2% of the time, Pallas kernels for 0%

profile of v1, /device:TPU:1, one launch (start us, length us, event | category | flops | bytes accessed | tf_op | source)
XLA Modules:
  0.0 215.0 jit_solution(12919904040907018257)
XLA Ops:
  7.2 0.7 convert_element_type.20
  7.9 0.8 copy.51
  8.7 0.1 eq.24
  8.7 0.1 convert_reduce_fusion
  8.9 0.1 pad.5.clone
  8.9 0.8 maximum_bitcast_fusion
  9.7 0.6 gather_fusion
  10.3 0.8 broadcast_select_fusion
  11.1 8.6 %all-to-all-start = ((f32[32,8,128]{2,1,0:T(8,128)}), f32[32,8,128]{2,1,0:T(8,128)S(1)}, u32[]{:S(2)}, u32[]{:S(2)}) async-start(f32[32,8,128]{2,1,0:T(8,128)} %broadcast_select_fusion), calls=%async_computation | async-start | bytes 262144 | tf_op jit(solution)/shard_map/all_to_all | solution.py:418
  19.7 0.8 fusion.4
  20.5 0.7 copy.54.center_ref
  21.2 0.8 copy.57.code_ref
  22.0 0.8 copy.56.view_ref
  22.8 0.9 copy.55.pos_ref
  23.7 3.5 %all-to-all-done.rays_ref = f32[32,8,128]{2,1,0:T(8,128)S(1)} async-done(((f32[32,8,128]{2,1,0:T(8,128)}), f32[32,8,128]{2,1,0:T(8,128)S(1)}, u32[]{:S(2)}, u32[]{:S(2)}) %all-to-all-start) | async-done | bytes 131104 | tf_op jit(solution)/shard_map/all_to_all | solution.py:418
  27.3 0.7 fusion.live_ref
  27.9 0.0 copy-start.1
  27.9 0.7 copy-done.1
  28.7 0.7 copy-done.3
  29.4 1.0 copy-done.5
  30.4 0.9 copy-done.6
  31.4 0.8 copy-done.8
  32.2 0.7 copy-done.10
  32.9 0.7 copy-done.12
  33.6 0.0 copy-start.13
  33.6 25.7 %forward_tiles.1 = (f32[32,4,128]{2,1,0:T(4,128)}, bf16[32,992,512]{2,1,0:T(8,128)(2,1)}, bf16[32,80,128]{2,1,0:T(8,128)(2,1)S(1)}, f32[32,8,512]{2,1,0:T(8,128)S(1)}) custom-call(s32[32]{0:T(128)S(1)} %fusion.live_ref, f32[3,1]{1,0:T(4,128)S(1)} %copy.54.center_ref, f32[32,8,128]{2,1,0:T(8,128)S(1)} %all-to-all-done.rays_ref, ...), custom_call_target="tpu_custom_call" | custom-call | flops 10000000000 | bytes 30000000 | tf_op jit(solution)/shard_map/forward_tiles/pallas_call | solution.py:336
  59.3 26.2 %all-to-all-start.1 = ((f32[32,4,128]{2,1,0:T(4,128)}), f32[32,4,128]{2,1,0:T(4,128)S(1)}, u32[]{:S(2)}, u32[]{:S(2)}) async-start(f32[32,4,128]{2,1,0:T(4,128)} %get-tuple-element.21), calls=%async_computation.1 | async-start | bytes 131072 | tf_op jit(solution)/shard_map/all_to_all | solution.py:424
  85.5 0.0 all-reduce.2.cloned.1.call-start
  85.5 7.3 %all-to-all-done.1 = f32[32,4,128]{2,1,0:T(4,128)S(1)} async-done(((f32[32,4,128]{2,1,0:T(4,128)}), f32[32,4,128]{2,1,0:T(4,128)S(1)}, u32[]{:S(2)}, u32[]{:S(2)}) %all-to-all-start.1) | async-done | bytes 65568 | tf_op jit(solution)/shard_map/all_to_all | solution.py:424
  92.8 0.6 gather_fusion.3
  93.3 0.6 gather_fusion.2
  93.9 0.6 gather_fusion.1
  94.5 0.0 copy-done.14
  94.5 0.6 multiply_reduce_fusion
  95.2 0.6 gather_fusion.4
  95.8 10.9 %all_to_all.15.cot_ref = f32[32,4,128]{2,1,0:T(4,128)S(1)} all-to-all(f32[32,4,128]{2,1,0:T(4,128)S(1)} %gather_fusion.4), channel_id=1, replica_groups=mesh['blk'=32,'rep'=4] {'blk'}, dimensions={0} | all-to-all | bytes 131072 | tf_op jit(solution)/shard_map/all_to_all | solution.py:430
  106.7 0.0 copy-done.11
  106.7 22.0 %backward_tiles.1 = f32[1984,256]{1,0:T(8,128)} custom-call(s32[32]{0:T(128)S(1)} %fusion.live_ref, f32[3,1]{1,0:T(4,128)S(1)} %copy.54.center_ref, f32[32,8,128]{2,1,0:T(8,128)S(1)} %all-to-all-done.rays_ref, f32[32,4,128]{2,1,0:T(4,128)S(1)} %all_to_all.15.cot_ref, bf16[32,992,512]{2,1,0:T(8,128)(2,1)} %get-tuple-element.22.saved_ref, ...), custom_call_target="tpu_custom_call" | custom-call | flops 20000000000 | bytes 30000000 | tf_op jit(solution)/shard_map/backward_tiles/pallas_call | solution.py:364
  128.6 0.0 copy-start.2
  128.6 0.0 copy-start.4
  128.7 0.0 all-reduce.2.cloned.1.call-update
  128.7 73.9 %all-reduce.2.cloned.1.call-done.g_ref = f32[1984,256]{1,0:T(8,128)} async-done(((f32[1984,256]{1,0:T(8,128)}), f32[1984,256]{1,0:T(8,128)}) %all-reduce.2.cloned.1.call-update) | async-done | bytes 2031632 | tf_op jit(solution)/shard_map/psum | solution.py:435
  202.5 1.6 copy-done
  204.1 1.4 unpack_gradients.1
  205.5 0.7 copy.60
  206.2 0.6 copy.63
  206.8 0.7 copy.61
  207.5 0.7 copy.62
  (29 shorter events, 0.1 us)
Async XLA Ops:
  11.1 16.2 %all-to-all-start = ((f32[32,8,128]{2,1,0:T(8,128)}), f32[32,8,128]{2,1,0:T(8,128)S(1)}, u32[]{:S(2)}, u32[]{:S(2)}) async-start(f32[32,8,128]{2,1,0:T(8,128)} %broadcast_select_fusion), calls=%async_computation | async-start | bytes 262144 | tf_op jit(solution)/shard_map/all_to_all | solution.py:418
  27.9 0.7 copy-start.1
  28.7 0.7 copy-start.3
  29.4 1.0 copy-start.5
  30.4 0.9 copy-start.6
  31.3 0.8 copy-start.8
  32.2 0.7 copy-start.10
  32.9 0.7 copy-start.12
  33.5 61.0 %copy-start.14 = (f32[3,640]{1,0:T(4,128)S(1)}, f32[3,640]{1,0:T(4,128)}, u32[]{:S(2)}) copy-start(f32[3,640]{1,0:T(4,128)} %param.22) | copy-start | bytes 23044
  33.5 73.1 %copy-start.7 = (bf16[1,2,256,256]{3,2,1,0:T(8,128)(2,1)S(1)}, bf16[1,2,256,256]{3,2,1,0:T(8,128)(2,1)}, u32[]{:S(2)}) copy-start(bf16[1,2,256,256]{3,2,1,0:T(8,128)(2,1)} %trunk_ref.3) | copy-start | bytes 786436
  33.6 73.1 %copy-start.9 = (bf16[1,128,256]{2,1,0:T(8,128)(2,1)S(1)}, bf16[1,128,256]{2,1,0:T(8,128)(2,1)}, u32[]{:S(2)}) copy-start(bf16[1,128,256]{2,1,0:T(8,128)(2,1)} %feature_ref.3) | copy-start | bytes 196612
  33.6 73.1 %copy-start.11 = (bf16[1,256]{1,0:T(2,128)(2,1)S(1)}, bf16[1,256]{1,0:T(2,128)(2,1)}, u32[]{:S(2)}) copy-start(bf16[1,256]{1,0:T(2,128)(2,1)} %density_ref.3) | copy-start | bytes 1540
  33.6 73.1 %copy-start.13 = (bf16[1,3,128]{2,1,0:T(4,128)(2,1)S(1)}, bf16[1,3,128]{2,1,0:T(4,128)(2,1)}, u32[]{:S(2)}) copy-start(bf16[1,3,128]{2,1,0:T(4,128)(2,1)} %radiance_ref.3) | copy-start | bytes 2308
  59.3 33.5 %all-to-all-start.1 = ((f32[32,4,128]{2,1,0:T(4,128)}), f32[32,4,128]{2,1,0:T(4,128)S(1)}, u32[]{:S(2)}, u32[]{:S(2)}) async-start(f32[32,4,128]{2,1,0:T(4,128)} %get-tuple-element.21), calls=%async_computation.1 | async-start | bytes 131072 | tf_op jit(solution)/shard_map/all_to_all | solution.py:424
  85.5 117.1 %all-reduce.2.cloned.1.call-start = ((), (), s32[]{:S(2)}) async-start(), calls=%async_computation.3 | async-start | bytes 4063232 | tf_op jit(solution)/shard_map/psum | solution.py:435
  128.6 73.9 %copy-start.2 = (bf16[63,96]{1,0:T(8,128)(2,1)S(1)}, bf16[63,96]{1,0:T(8,128)(2,1)}, u32[]{:S(2)}) copy-start(bf16[63,96]{1,0:T(8,128)(2,1)} %constant.32.clone.pos_select_ref) | copy-start | bytes 36292
  128.6 73.9 %copy-start.4 = (bf16[27,48]{1,0:T(8,128)(2,1)S(1)}, bf16[27,48]{1,0:T(8,128)(2,1)}, u32[]{:S(2)}) copy-start(bf16[27,48]{1,0:T(8,128)(2,1)} %constant.33.clone.view_select_ref) | copy-start | bytes 7780
  202.5 1.6 copy-start
Sparse Core Ops, SparseCore 0:
  128.8 73.6 all-reduce.1

commit v2 on v1

--- a/solution.py
+++ b/solution.py
@@ -32,9 +32,11 @@
 G_T1 = 0
 G_T2 = 256
 G_FD = 512
-G_TAB = 656
-G_POS = 1680
-G_ROWS = 1984
+G_TAB = 640
+G_POS = 1664
+G_RAD = G_POS + 128
+G_DEN = G_RAD + 16
+G_ROWS = 1920
 
 
 def code_places(levels, half):
@@ -292,7 +294,10 @@
         )
         g_ref[G_TAB:G_POS, :] += mm_nt(spread, hot)
         both = jnp.concatenate([d_feature.astype(jnp.bfloat16), d_small], 0)
-        g_ref[G_FD:G_TAB, :] += mm_nt(both, act[R_H3:R_S, :])
+        d_both = mm_nt(both, act[R_H3:R_S, :])
+        g_ref[G_FD:G_TAB, :] += d_both[:CHID]
+        g_ref[G_DEN : G_DEN + 16, 128:256] += d_both[CHID:, :128]
+        g_ref[G_DEN + 16 : G_DEN + 32, 128:256] += d_both[CHID:, 128:]
         d_z = through(mm(fdt[...], both), R_H3, R_S).astype(jnp.bfloat16)
         g_ref[G_T2:G_FD, :] += mm_nt(d_z, act[R_H2:R_H3, :])
         d_z = through(mm(t2[...], d_z), R_H2, R_H3).astype(jnp.bfloat16)
@@ -318,7 +323,8 @@
     trunk_ref[0, 0] = g_ref[G_T1:G_T2, :]
     trunk_ref[0, 1] = g_ref[G_T2:G_FD, :]
     feature_ref[0] = g_ref[G_FD : G_FD + CHID, :]
-    density_ref[...] = g_ref[G_FD + CHID + 3 : G_FD + CHID + 4, :]
+    density_ref[:, :128] = g_ref[G_DEN + 3 : G_DEN + 4, 128:256]
+    density_ref[:, 128:] = g_ref[G_DEN + 19 : G_DEN + 20, 128:256]
     view_ref[0] = pick(g_ref[G_POS : G_POS + CHID, 128 : 128 + VC], view_select_ref[...])
     code_ref[0] = g_ref[G_POS : G_POS + CHID, 128 + VC : 128 + RC]
     radiance_ref[0] = g_ref[G_POS + CHID : G_POS + CHID + 3, 128:256]
@@ -396,6 +402,171 @@
     )(packed, jnp.asarray(POS_SELECT, jnp.bfloat16), jnp.asarray(VIEW_SELECT, jnp.bfloat16))
 
 
+MESH = pl.DeviceIdType.MESH
+GROUP = SLOTS
+REPS = 4
+CHUNK = G_ROWS // (4 * REPS)
+
+
+def place():
+    return lax.axis_index("blk"), lax.axis_index("rep")
+
+
+def partner(blk, rep, i):
+    return lax.rem(blk + i, GROUP), lax.rem(rep + GROUP * REPS - i, REPS)
+
+
+def meet(blk, rep):
+    barrier = pltpu.get_barrier_semaphore()
+
+    def greet(i, carry):
+        pl.semaphore_signal(barrier, inc=1, device_id=partner(blk, rep, i), device_id_type=MESH)
+        return carry
+
+    lax.fori_loop(1, GROUP, greet, 0)
+    pl.semaphore_wait(barrier, GROUP - 1)
+
+
+def exchange(blk, rep, src, dst, send_sem, recv_sem):
+    def copy(i):
+        to_blk, to_rep = partner(blk, rep, i)
+        return pltpu.make_async_remote_copy(
+            src_ref=src.at[to_blk], dst_ref=dst.at[blk], send_sem=send_sem.at[i],
+            recv_sem=recv_sem.at[i], device_id=(to_blk, to_rep), device_id_type=MESH,
+        )
+
+    def begin(i, carry):
+        copy(i).start()
+        return carry
+
+    lax.fori_loop(1, GROUP, begin, 0)
+    dst[blk] = src[blk]
+    return copy
+
+
+def finish(copy):
+    def end(i, carry):
+        copy(i).wait()
+        return carry
+
+    lax.fori_loop(1, GROUP, end, 0)
+
+
+def scatter_kernel(tile_ref, live_ref, tiles_ref, out_ref, send, send_sem, recv_sem):
+    blk, rep = place()
+    row = row_iota(8, TILE)
+    for k in range(GROUP):
+        flag = live_ref[k].astype(jnp.float32)
+        send[k] = jnp.where(row == 7, flag, tiles_ref[tile_ref[k]])
+    meet(blk, rep)
+    finish(exchange(blk, rep, send, out_ref, send_sem, recv_sem))
+
+
+def blend_kernel(
+    ids_ref, tile_ref, part_ref, grad_ref, colors_ref, cot_ref,
+    back, cots, send, send_sem, recv_sem, send_sem2, recv_sem2,
+):
+    blk, rep = place()
+    meet(blk, rep)
+    finish(exchange(blk, rep, part_ref, back, send_sem, recv_sem))
+    for t in range(cots.shape[0]):
+        summed = back[ids_ref[3 * t]] + back[ids_ref[3 * t + 1]] + back[ids_ref[3 * t + 2]]
+        lanes = slice(t * TILE, (t + 1) * TILE)
+        colors = summed[:3] / summed[3:4]
+        colors_ref[:, lanes] = colors
+        cot = grad_ref[:, lanes] * LOSS_SCALE / summed[3:4]
+        cots[t] = jnp.concatenate([cot, -jnp.sum(cot * colors, 0, keepdims=True)], 0)
+    for k in range(GROUP):
+        send[k] = cots[tile_ref[k]]
+    finish(exchange(blk, rep, send, cot_ref, send_sem2, recv_sem2))
+
+
+def total_kernel(g_ref, out_ref, got, held, send_sem, recv_sem):
+    blk, rep = place()
+    up, down = lax.rem(rep + 1, REPS), lax.rem(rep + REPS - 1, REPS)
+    barrier = pltpu.get_barrier_semaphore()
+    for other in (up, down):
+        pl.semaphore_signal(barrier, inc=1, device_id=(blk, other), device_id_type=MESH)
+    pl.semaphore_wait(barrier, 2)
+    rings = range(4)
+
+    def chunk(ring, ahead):
+        sign = 1 if ring % 2 == 0 else REPS - 1
+        which = lax.rem(rep + sign * (ahead + REPS), REPS)
+        return pl.ds(pl.multiple_of((ring * REPS + which) * CHUNK, 8), CHUNK)
+
+    def copy(ring, step):
+        if step == 0:
+            src, dst = g_ref.at[chunk(ring, 0)], got.at[ring, 0]
+        elif step < 3:
+            src, dst = held.at[ring, step - 1], got.at[ring, step]
+        else:
+            rows = chunk(ring, 4 - step)
+            src, dst = out_ref.at[rows], out_ref.at[rows]
+        return pltpu.make_async_remote_copy(
+            src_ref=src, dst_ref=dst, send_sem=send_sem.at[ring, step],
+            recv_sem=recv_sem.at[ring, step],
+            device_id=(blk, up if ring % 2 == 0 else down), device_id_type=MESH,
+        )
+
+    for ring in rings:
+        copy(ring, 0).start()
+    for step in range(6):
+        for ring in rings:
+            copy(ring, step).wait_recv()
+            if step < 2:
+                held[ring, step] = got[ring, step] + g_ref[chunk(ring, -step - 1), :]
+            elif step == 2:
+                out_ref[chunk(ring, 1), :] = got[ring, 2] + g_ref[chunk(ring, 1), :]
+            if step < 5:
+                copy(ring, step + 1).start()
+    for step in range(6):
+        for ring in rings:
+            copy(ring, step).wait_send()
+
+
+def communicate(kernel, name, number, args, specs, shapes, scratch):
+    return pl.pallas_call(
+        kernel,
+        name=name,
+        out_shape=shapes,
+        in_specs=specs,
+        out_specs=jax.tree.map(lambda _: VMEM, shapes),
+        scratch_shapes=scratch,
+        compiler_params=pltpu.CompilerParams(
+            collective_id=number, has_side_effects=True, vmem_limit_bytes=16 * 1024 * 1024
+        ),
+    )(*args)
+
+
+def run_scatter(tile_of, live, tiles):
+    return communicate(
+        scatter_kernel, "scatter_rays", 0, (tile_of, live, tiles), [SMEM, SMEM, VMEM],
+        jax.ShapeDtypeStruct((GROUP, 8, TILE), jnp.float32),
+        [pltpu.VMEM((GROUP, 8, TILE), jnp.float32)] + [pltpu.SemaphoreType.DMA((GROUP,))] * 2,
+    )
+
+
+def run_blend(ids, tile_of, part, grad):
+    tiles = grad.shape[1] // TILE
+    small = (GROUP, 4, TILE)
+    return communicate(
+        blend_kernel, "blend_colors", 1, (ids, tile_of, part, grad), [SMEM, SMEM, VMEM, VMEM],
+        (jax.ShapeDtypeStruct(grad.shape, jnp.float32), jax.ShapeDtypeStruct(small, jnp.float32)),
+        [pltpu.VMEM(small, jnp.float32), pltpu.VMEM((tiles, 4, TILE), jnp.float32),
+         pltpu.VMEM(small, jnp.float32)] + [pltpu.SemaphoreType.DMA((GROUP,))] * 4,
+    )
+
+
+def run_total(packed):
+    return communicate(
+        total_kernel, "total_gradients", 2, (packed,), [VMEM],
+        jax.ShapeDtypeStruct((G_ROWS, 256), jnp.float32),
+        [pltpu.VMEM((4, 3, CHUNK, 256), jnp.float32), pltpu.VMEM((4, 2, CHUNK, 256), jnp.float32)]
+        + [pltpu.SemaphoreType.DMA((4, 6))] * 2,
+    )
+
+
 def local(
     anchors, directions, app_ids, block_ids, color_grad, block_centers, pos_weight, trunk_weight,
     density_weight, feature_weight, view_weight, code_weight, radiance_weight, code_table,
@@ -410,30 +581,18 @@
         [anchors, directions, app_ids.astype(jnp.float32)[None], jnp.zeros((1, tiles * TILE), jnp.float32)], 0
     )
     ray_tiles = rows.reshape(8, tiles, TILE).transpose(1, 0, 2)
-    send = jnp.where(
-        jnp.arange(8)[None, :, None] == 7,
-        is_live.astype(jnp.float32)[:, None, None],
-        ray_tiles[source_tile],
-    )
-    rays = lax.all_to_all(send, "blk", split_axis=0, concat_axis=0, tiled=True)
+    rays = run_scatter(source_tile, is_live, ray_tiles)
     live = (rays[:, 7, 0] > 0.5).astype(jnp.int32)
     part, saved, raycode, small = run_forward(
         live, block_centers, rays, pos_weight, trunk_weight, density_weight, feature_weight,
         view_weight, code_weight, radiance_weight, code_table,
     )
-    returned = lax.all_to_all(part, "blk", split_axis=0, concat_axis=0, tiled=True)
-    summed = returned[block_ids[:, 0]] + returned[block_ids[:, 1]] + returned[block_ids[:, 2]]
-    scaled = color_grad.reshape(3, tiles, TILE).transpose(1, 0, 2) * LOSS_SCALE
-    colors = summed[:, :3] / summed[:, 3:4]
-    cot_color = scaled / summed[:, 3:4]
-    cot = jnp.concatenate([cot_color, -jnp.sum(cot_color * colors, 1, keepdims=True)], 1)
-    got_cot = lax.all_to_all(cot[source_tile], "blk", split_axis=0, concat_axis=0, tiled=True)
+    colors, cot = run_blend(flat_ids, source_tile, part, color_grad)
     packed = run_backward(
-        live, block_centers, rays, got_cot, saved, raycode, small, trunk_weight, density_weight,
+        live, block_centers, rays, cot, saved, raycode, small, trunk_weight, density_weight,
         feature_weight, code_weight, radiance_weight,
     )
-    packed = lax.psum(packed, "rep")
-    return (colors.transpose(1, 0, 2).reshape(3, tiles * TILE),) + tuple(run_unpack(packed))
+    return (colors,) + tuple(run_unpack(run_total(packed)))
 
 
 def solution(mesh):

time: 217 us -> 148 us (0.68)
  waiting for transfers between devices: 84.7 us -> 0 us
  Pallas kernels: 49.1 us -> 129 us
  starting transfers between devices: 34.8 us -> 0 us
  between operations: 14.2 us -> 0.79 us
  blocking collectives: 10.9 us -> 0 us
  local copies, waits for them, and re-layouts: 17 us -> 13.1 us
  other arithmetic: 4.47 us -> 2.24 us
    pallas_call x0 -> x3, Pallas kernels: none -> 76.6 us  [communicate(): pl.pallas_call(kernel, name=name, out_shape=shapes, in_specs=specs, out_s...]
    psum x1 -> x0, waiting for transfers between devices: 73.9 us -> none  [local(): packed = lax.psum(packed, 'rep')]
    all_to_all x2 -> x0, starting transfers between devices: 34.7 us -> none  [the longest x1 26.2 us: local(): lax.all_to_all(part, 'blk', split_axis=0, concat_axis=0, tiled=True)]
    all_to_all x1 -> x0, blocking collectives: 10.9 us -> none  [local(): lax.all_to_all(cot[source_tile], 'blk', split_axis=0, concat_axis=0, tile...]
    all_to_all x2 -> x0, waiting for transfers between devices: 10.8 us -> none  [the longest x1 7.26 us: local(): lax.all_to_all(part, 'blk', split_axis=0, concat_axis=0, tiled=True)]
    gather x5 -> x0, local copies, waits for them, and re-layouts: 2.9 us -> none  [the longest x1 0.61 us: local(): cot[source_tile]]
    pallas_call x1, Pallas kernels: 25.7 us -> 28.1 us  [run_forward(): pl.pallas_call(forward_kernel, name='forward_tiles', out_shape=(jax.Shape...]
    unnamed x40 -> x38, local copies, waits for them, and re-layouts: 13.9 us -> 12.9 us
  transfers between devices with their start and end apart: 3 -> 0, of which waited for: 3 -> 0; matrix products, arithmetic and copies ran while one was open for 2% -> 0% of each run, Pallas kernels for 0% -> 0%
where the time goes in v2:
time: 148 us; the launch traced here: 145 us
  Pallas kernels  129 us (87%)
  local copies, waits for them, and re-layouts  13.1 us (9%)
  other arithmetic  2.24 us (2%)
    pallas_call x3, Pallas kernels, communicate(): pl.pallas_call(kernel, name=name, out_shape=shapes, in_specs=specs, out_s...  76.6 us
    pallas_call x1, Pallas kernels, run_forward(): pl.pallas_call(forward_kernel, name='forward_tiles', out_shape=(jax.Shape...  28.1 us
    pallas_call x1, Pallas kernels, run_backward(): pl.pallas_call(backward_kernel, name='backward_tiles', out_shape=jax.Shap...  23.1 us
    unnamed x38, local copies, waits for them, and re-layouts  12.9 us

profile of v2, /device:TPU:1, one launch (start us, length us, event | category | flops | bytes accessed | tf_op | source)
XLA Modules:
  0.0 145.3 jit_solution(12227672626004836953)
XLA Ops:
  0.6 0.8 copy.49
  1.4 0.1 reshape.32.ids_ref
  1.5 0.1 convert_reduce_fusion
  1.6 0.7 convert_element_type.12
  2.3 0.1 pad.3.clone
  2.4 0.8 maximum_bitcast_fusion.tiles_ref
  3.2 15.9 %scatter_rays.1.rays_ref = f32[32,8,128]{2,1,0:T(8,128)S(1)} custom-call(s32[32]{0:T(128)S(1)} %and_select_fusion.tile_ref, s32[32]{0:T(128)S(1)} %get-tuple-element.64.live_ref, f32[5,8,128]{2,1,0:T(8,128)S(1)} %maximum_bitcast_fusion.tiles_ref), custom_call_target="tpu_custom_call" | custom-call | tf_op jit(solution)/shard_map/scatter_rays/pallas_call | solution.py:529
  19.1 0.7 fusion.live_ref
  19.8 0.8 copy.50.center_ref
  20.5 0.9 copy.51.pos_ref
  21.4 0.8 copy.52.view_ref
  22.2 0.8 copy.53.code_ref
  23.0 0.0 copy-start
  23.0 0.7 copy-done
  23.8 0.0 copy-start.3
  23.8 0.7 copy-done.3
  24.5 0.0 copy-start.5
  24.5 1.0 copy-done.5
  25.5 0.0 copy-start.6
  25.5 0.9 copy-done.6
  26.4 0.0 copy-start.8
  26.4 0.8 copy-done.8
  27.3 0.0 copy-start.10
  27.3 0.7 copy-done.10
  28.0 0.0 copy-start.12
  28.0 0.7 copy-done.12
  28.6 0.0 copy-start.2
  28.6 0.0 copy-start.7
  28.7 0.0 copy-start.13
  28.7 28.1 %forward_tiles.1 = (f32[32,4,128]{2,1,0:T(4,128)S(1)}, bf16[32,992,512]{2,1,0:T(8,128)(2,1)}, bf16[32,80,128]{2,1,0:T(8,128)(2,1)S(1)}, f32[32,8,512]{2,1,0:T(8,128)S(1)}) custom-call(s32[32]{0:T(128)S(1)} %fusion.live_ref, f32[3,1]{1,0:T(4,128)S(1)} %copy.50.center_ref, f32[32,8,128]{2,1,0:T(8,128)S(1)} %scatter_rays.1.rays_ref, ...), custom_call_target="tpu_custom_call" | custom-call | flops 10000000000 | bytes 30000000 | tf_op jit(solution)/shard_map/forward_tiles/pallas_call | solution.py:342
  56.8 0.0 copy-done.2
  56.8 25.2 %blend_colors.1 = (f32[3,640]{1,0:T(4,128)S(1)}, f32[32,4,128]{2,1,0:T(4,128)S(1)}) custom-call(s32[15]{0:T(128)S(1)} %reshape.32.ids_ref, s32[32]{0:T(128)S(1)} %and_select_fusion.tile_ref, f32[32,4,128]{2,1,0:T(4,128)S(1)} %get-tuple-element.23.part_ref, f32[3,640]{1,0:T(4,128)S(1)} %copy-done.2), custom_call_target="tpu_custom_call" | custom-call | tf_op jit(solution)/shard_map/blend_colors/pallas_call | solution.py:529
  82.0 0.0 copy-done.7
  82.0 0.0 copy-done.9
  82.0 0.0 copy-done.11
  82.0 0.0 copy-done.13
  82.0 23.1 %backward_tiles.1.g_ref = f32[1920,256]{1,0:T(8,128)S(1)} custom-call(s32[32]{0:T(128)S(1)} %fusion.live_ref, f32[3,1]{1,0:T(4,128)S(1)} %copy.50.center_ref, f32[32,8,128]{2,1,0:T(8,128)S(1)} %scatter_rays.1.rays_ref, f32[32,4,128]{2,1,0:T(4,128)S(1)} %get-tuple-element.25.cot_ref, bf16[32,992,512]{2,1,0:T(8,128)(2,1)} %get-tuple-element.26.saved_ref, ...), custom_call_target="tpu_custom_call" | custom-call | flops 20000000000 | bytes 30000000 | tf_op jit(solution)/shard_map/backward_tiles/pallas_call | solution.py:370
  105.1 0.0 copy-start.1
  105.2 0.0 copy-start.4
  105.2 35.5 %total_gradients.1.g_ref = f32[1920,256]{1,0:T(8,128)S(1)} custom-call(f32[1920,256]{1,0:T(8,128)S(1)} %backward_tiles.1.g_ref), custom_call_target="tpu_custom_call" | custom-call | tf_op jit(solution)/shard_map/total_gradients/pallas_call | solution.py:529
  140.6 0.0 copy-done.1
  140.6 0.0 copy-done.4
  140.6 1.4 unpack_gradients.1
  142.1 0.7 copy.56
  142.8 0.7 copy.57
  143.5 0.7 copy.58
  144.1 0.6 copy.59
  144.7 0.6 copy.61
  (4 shorter events, 0.0 us)
Async XLA Ops:
  23.0 0.7 copy-start
  23.8 0.7 copy-start.3
  24.5 1.0 copy-start.5
  25.5 0.9 copy-start.6
  26.4 0.8 copy-start.8
  27.3 0.7 copy-start.10
  28.0 0.7 copy-start.12
  28.6 28.1 %copy-start.2 = (f32[3,640]{1,0:T(4,128)S(1)}, f32[3,640]{1,0:T(4,128)}, u32[]{:S(2)}) copy-start(f32[3,640]{1,0:T(4,128)} %grad_ref.1) | copy-start | bytes 23044
  28.6 53.3 %copy-start.7 = (bf16[1,2,256,256]{3,2,1,0:T(8,128)(2,1)S(1)}, bf16[1,2,256,256]{3,2,1,0:T(8,128)(2,1)}, u32[]{:S(2)}) copy-start(bf16[1,2,256,256]{3,2,1,0:T(8,128)(2,1)} %trunk_ref.3) | copy-start | bytes 786436
  28.6 53.3 %copy-start.9 = (bf16[1,128,256]{2,1,0:T(8,128)(2,1)S(1)}, bf16[1,128,256]{2,1,0:T(8,128)(2,1)}, u32[]{:S(2)}) copy-start(bf16[1,128,256]{2,1,0:T(8,128)(2,1)} %feature_ref.3) | copy-start | bytes 196612
  28.7 53.3 %copy-start.11 = (bf16[1,256]{1,0:T(2,128)(2,1)S(1)}, bf16[1,256]{1,0:T(2,128)(2,1)}, u32[]{:S(2)}) copy-start(bf16[1,256]{1,0:T(2,128)(2,1)} %density_ref.3) | copy-start | bytes 1540
  28.7 53.3 %copy-start.13 = (bf16[1,3,128]{2,1,0:T(4,128)(2,1)S(1)}, bf16[1,3,128]{2,1,0:T(4,128)(2,1)}, u32[]{:S(2)}) copy-start(bf16[1,3,128]{2,1,0:T(4,128)(2,1)} %radiance_ref.3) | copy-start | bytes 2308
  105.1 35.5 %copy-start.1 = (bf16[63,96]{1,0:T(8,128)(2,1)S(1)}, bf16[63,96]{1,0:T(8,128)(2,1)}, u32[]{:S(2)}) copy-start(bf16[63,96]{1,0:T(8,128)(2,1)} %constant.21.clone.pos_select_ref) | copy-start | bytes 36292
  105.2 35.5 %copy-start.4 = (bf16[27,48]{1,0:T(8,128)(2,1)S(1)}, bf16[27,48]{1,0:T(8,128)(2,1)}, u32[]{:S(2)}) copy-start(bf16[27,48]{1,0:T(8,128)(2,1)} %constant.22.clone.view_select_ref) | copy-start | bytes 7780
